TPU v7x, 256 devices: a 4x2x16 block of a 4x16x16 slice. The times are simulated.
256 devices in a mesh: groups: 2 (over y), ctx: 16 (over z), fsdp: 8 (over x, core).
Axes of the slice: x: 4, y: 2, z: 16, core: 2. Of those that a mesh axis runs over, the one named last changes fastest.
The devices are a block of a 4x16x16 slice.
Arguments:
- patches: bfloat16 [16, 4096, 1024], P(('groups', 'fsdp'), 'ctx'), parts along dimension 0, may hold values from -6 to 6
- segment_ids: int32 [16, 4096], P(('groups', 'fsdp'), 'ctx'), parts along dimension 0, may hold values from 0 to 15, never falling along the last dimension, each value on 1 to 3072 neighbouring positions
- patch_rows: int32 [16, 4096], P(('groups', 'fsdp'), 'ctx'), parts along dimension 0, may hold values from 0 to 63
- patch_cols: int32 [16, 4096], P(('groups', 'fsdp'), 'ctx'), parts along dimension 0, may hold values from 0 to 63
- row_table: bfloat16 [64, 1024], replicated, may hold values from -3 to 3
- col_table: bfloat16 [64, 1024], replicated, may hold values from -3 to 3
- norm_gain: float32 [1024], replicated, may hold values from 0.1 to 1.9
- qkv_weight: bfloat16 [1024, 3072], P('fsdp'), may hold values from -5 to 5
- out_weight: bfloat16 [1024, 1024], P(None, 'fsdp'), may hold values from -0.1875 to 0.1875
Outputs:
- encoded: bfloat16 [16, 4096, 1024], P(('groups', 'fsdp'), 'ctx'), parts along dimension 0
There are 2 independent parts, one for each index of `groups`. A program takes and returns all parts, laid end to end along the dimension named above; an argument that names none is the same for every part. Nothing has to cross between parts.
All inputs are finite; a program needn't handle non-finite values.
Results may differ from a plain program's by a relative error of at most 0.0044.
The roundings to bfloat16 on the way count: a program that leaves them out, or rounds other values in their place, can miss the bound.
Values may be sent and summed in bfloat16 or wider, within the bound.
A program may use at most 64 MiB of HBM per device.

v0:
```python
import jax
import jax.numpy as jnp
from jax import lax
from jax.sharding import Mesh
from jax.sharding import PartitionSpec as P

HEADS = 16
FSDP = ("fsdp_0", "fsdp_1")
GROUPS_FSDP = ("groups", "fsdp_0", "fsdp_1")
floor_score = -1e30
epsilon = 1e-06


def laid_out(blocks, dim):
    lengths = list(blocks.shape[1:])
    lengths[dim] *= blocks.shape[0]
    return jnp.moveaxis(blocks, 0, dim).reshape(lengths)


def sent_to_all(value, axis):
    copies = jnp.broadcast_to(value, (lax.axis_size(axis), *value.shape))
    return lax.all_to_all(copies, axis, split_axis=0, concat_axis=0, tiled=True)


def collect(value, axis, dim):
    return laid_out(sent_to_all(value, axis), dim)


def edges_of(length, count):
    unit = 8 if length >= 8 * count else 1
    return [length // unit * k // count * unit for k in range(1, count)]


def stacked_from(value, axes, order):
    blocks = value[None]
    for k in order:
        blocks = lax.all_gather(blocks, axes[k], axis=0, tiled=True)
    block = [lax.axis_size(axes[k]) for k in reversed(order)]
    blocks = blocks.reshape(*block, *value.shape)
    turned = sorted(range(len(order)), key=lambda place: order[len(order) - 1 - place])
    return blocks.transpose(*turned, *range(len(order), blocks.ndim)).reshape(-1, *value.shape)


def spread_gather(value, axes, dim):
    cut = max(range(max(1, value.ndim - 1)), key=lambda d: value.shape[d])
    count, done = (len(axes), [])
    for initial, section in enumerate(
        jnp.split(value, edges_of(value.shape[cut], count), axis=cut)
    ):
        if section.size:
            order = [(initial - k) % count for k in range(count)]
            done.append(stacked_from(section, axes, order))
    return laid_out(jnp.concatenate(done, axis=cut + 1), dim)


def body(
    patches,
    segment_ids,
    patch_rows,
    patch_cols,
    row_table,
    col_table,
    norm_gain,
    qkv_weight,
    out_weight,
):
    tokens = patches[0]
    labels = segment_ids[0]
    model_width = tokens.shape[1]
    head_count = HEADS
    head_size = model_width // head_count
    score_scale = 1.0 / head_size**0.5
    grid_size = row_table.shape[0]
    levels = lax.broadcasted_iota(jnp.int32, (1, grid_size), 1)
    row_onehot = (patch_rows[0][:, None] == levels).astype(jnp.bfloat16)
    col_onehot = (patch_cols[0][:, None] == levels).astype(jnp.bfloat16)
    embedded = (
        tokens.astype(jnp.float32)
        + jnp.dot(row_onehot, row_table, preferred_element_type=jnp.float32)
        + jnp.dot(col_onehot, col_table, preferred_element_type=jnp.float32)
    )
    average = jnp.mean(embedded, axis=-1, keepdims=True)
    centered = embedded - average
    variance = jnp.mean(centered * centered, axis=-1, keepdims=True)
    normed = (centered * lax.rsqrt(variance + epsilon) * norm_gain).astype(jnp.bfloat16)
    qkv = jnp.dot(
        normed,
        lax.all_gather(qkv_weight, FSDP, axis=0, tiled=True),
        preferred_element_type=jnp.float32,
    ).astype(jnp.bfloat16)
    queries = qkv[:, :model_width]
    key_rows = qkv[:, model_width : 2 * model_width]
    value_rows = qkv[:, 2 * model_width :]
    query_part, key_part, value_part = (
        lax.all_to_all(queries, "ctx", split_axis=1, concat_axis=0, tiled=True),
        lax.all_to_all(key_rows, "ctx", split_axis=1, concat_axis=0, tiled=True),
        lax.all_to_all(value_rows, "ctx", split_axis=1, concat_axis=0, tiled=True),
    )
    full_labels = collect(labels, "ctx", 0)
    full_length = query_part.shape[0]
    local_width = query_part.shape[1]
    local_heads = local_width // head_size
    span = min(512, full_length)
    key_heads = key_part.reshape(full_length, local_heads, head_size)
    value_heads = value_part.reshape(full_length, local_heads, head_size)

    def attend_span(offset):
        span_rows = lax.dynamic_slice_in_dim(query_part, offset, span, 0).reshape(
            span, local_heads, head_size
        )
        span_labels = lax.dynamic_slice_in_dim(full_labels, offset, span, 0)
        scores = (
            jnp.einsum("qhd,khd->hqk", span_rows, key_heads, preferred_element_type=jnp.float32)
            * score_scale
        )
        same_segment = (span_labels[:, None] == full_labels[None, :])[None]
        masked = jnp.where(same_segment, scores, floor_score)
        highest = jnp.max(masked, axis=-1, keepdims=True)
        raised = jnp.where(same_segment, jnp.exp(masked - highest), 0.0)
        row_sums = jnp.sum(raised, axis=-1)
        mixed = jnp.einsum(
            "hqk,khd->qhd",
            raised.astype(jnp.bfloat16),
            value_heads,
            preferred_element_type=jnp.float32,
        )
        mixed = mixed / row_sums.T[:, :, None]
        return mixed.reshape(span, local_width).astype(jnp.bfloat16)

    offsets = jnp.arange(full_length // span, dtype=jnp.int32) * span
    head_context = lax.map(attend_span, offsets).reshape(full_length, local_width)
    context = lax.all_to_all(head_context, "ctx", split_axis=0, concat_axis=1, tiled=True)
    attended = jnp.dot(
        context, spread_gather(out_weight, FSDP, 1), preferred_element_type=jnp.float32
    )
    encoded = (embedded + attended).astype(jnp.bfloat16)
    return encoded[None]


def solution(mesh):
    finer = Mesh(
        mesh.devices.reshape(mesh.shape["groups"], mesh.shape["ctx"], 4, 2),
        ("groups", "ctx", "fsdp_0", "fsdp_1"),
    )
    placed = (
        P(GROUPS_FSDP, "ctx", None),
        P(GROUPS_FSDP, "ctx"),
        P(GROUPS_FSDP, "ctx"),
        P(GROUPS_FSDP, "ctx"),
        P(),
        P(),
        P(),
        P(FSDP, None),
        P(None, FSDP),
    )
    return jax.shard_map(
        body, mesh=finer, in_specs=placed, out_specs=P(GROUPS_FSDP, "ctx", None), check_vma=False
    )
```

profile of v0, /device:TPU:40, one launch (start us, length us, event | category | flops | bytes accessed | tf_op | source)
XLA Modules:
  0.0 326.7 jit_solution(15467032216599425548)
XLA Ops:
  9.5 24.0 %all-to-all-start = ((s32[16,1,256]{2,1,0:T(1,128)}), s32[16,1,256]{2,1,0:T(1,128)S(1)}, u32[]{:S(2)}, u32[]{:S(2)}) async-start(s32[16,1,256]{2,1,0:T(1,128)} %broadcast_in_dim.31), calls=%async_computation | async-start | bytes 32768 | tf_op jit(solution)/shard_map/all_to_all | solution.py:22
  36.3 33.9 %all-gather.6.cloned.1.call-done = bf16[1024,3072]{1,0:T(8,128)(2,1)} async-done(((bf16[128,3072]{1,0:T(8,128)(2,1)}), bf16[1024,3072]{1,0:T(8,128)(2,1)}) %all-gather.6.cloned.1.call-update) | async-done | bytes 6291472 | tf_op jit(solution)/shard_map/all_gather | solution.py:88
  70.2 4.7 %convolution_convert_fusion = bf16[256,3072]{1,0:T(8,128)(2,1)S(1)} fusion(bf16[1024,3072]{1,0:T(8,128)(2,1)} %all-gather.6.cloned.1.call-done, f32[256,1024]{1,0:T(8,128)S(1)} %get-tuple-element.96, f32[1024]{0:T(1024)} %param.17, f32[256]{0:T(256)S(1)} %add_rsqrt_fusion, f32[256]{0:T(256)S(1)} %broadcast_multiply_fusion), kind=kOutput, calls=%fused_computation.19 | convolution fusion | flops 1612447744 | bytes 8919040 | tf_op jit(solution)/shard_map/dot_general | solution.py:86
  76.1 12.4 %all-to-all-start.1 = ((bf16[256,16,64]{0,2,1:T(8,128)(2,1)}), bf16[256,16,64]{0,2,1:T(8,128)(2,1)S(1)}, u32[]{:S(2)}, u32[]{:S(2)}) async-start(bf16[256,16,64]{0,2,1:T(8,128)(2,1)} %bitcast.12), calls=%async_computation.1 | async-start | bytes 1048576 | tf_op jit(solution)/shard_map/all_to_all | solution.py:95
  89.4 28.0 %all-to-all-done.1 = bf16[256,16,64]{0,2,1:T(8,128)(2,1)S(1)} async-done(((bf16[256,16,64]{0,2,1:T(8,128)(2,1)}), bf16[256,16,64]{0,2,1:T(8,128)(2,1)S(1)}, u32[]{:S(2)}, u32[]{:S(2)}) %all-to-all-start.1) | async-done | bytes 524320 | tf_op jit(solution)/shard_map/all_to_all | solution.py:95
  117.5 6.8 %all-to-all-start.2 = ((bf16[256,16,64]{0,2,1:T(8,128)(2,1)}), bf16[256,16,64]{0,2,1:T(8,128)(2,1)S(1)}, u32[]{:S(2)}, u32[]{:S(2)}) async-start(bf16[256,16,64]{0,2,1:T(8,128)(2,1)} %bitcast.15), calls=%async_computation.2 | async-start | bytes 1048576 | tf_op jit(solution)/shard_map/all_to_all | solution.py:96
  125.3 27.9 %all-to-all-done.2 = bf16[256,16,64]{0,2,1:T(8,128)(2,1)S(1)} async-done(((bf16[256,16,64]{0,2,1:T(8,128)(2,1)}), bf16[256,16,64]{0,2,1:T(8,128)(2,1)S(1)}, u32[]{:S(2)}, u32[]{:S(2)}) %all-to-all-start.2) | async-done | bytes 524320 | tf_op jit(solution)/shard_map/all_to_all | solution.py:96
  153.2 6.6 %all-to-all-start.3 = ((bf16[256,16,64]{0,2,1:T(8,128)(2,1)}), bf16[256,16,64]{0,2,1:T(8,128)(2,1)S(1)}, u32[]{:S(2)}, u32[]{:S(2)}) async-start(bf16[256,16,64]{0,2,1:T(8,128)(2,1)} %bitcast.17), calls=%async_computation.3 | async-start | bytes 1048576 | tf_op jit(solution)/shard_map/all_to_all | solution.py:97
  160.0 14.4 %all-gather = bf16[2048,128]{1,0:T(8,128)(2,1)} all-gather(bf16[512,128]{1,0:T(8,128)(2,1)S(1)} %get-tuple-element.93), channel_id=2, replica_groups=mesh['groups'=2,'ctx'=16,'fsdp_0'=4,'fsdp_1'=2] {'fsdp_0'}, dimensions={0}, use_global_device_ids=true | all-gather | bytes 655360 | tf_op jit(solution)/shard_map/all_gather | solution.py:37
  176.3 12.4 %all-to-all-done.3 = bf16[256,16,64]{0,2,1:T(8,128)(2,1)S(1)} async-done(((bf16[256,16,64]{0,2,1:T(8,128)(2,1)}), bf16[256,16,64]{0,2,1:T(8,128)(2,1)S(1)}, u32[]{:S(2)}, u32[]{:S(2)}) %all-to-all-start.3) | async-done | bytes 524320 | tf_op jit(solution)/shard_map/all_to_all | solution.py:97
  189.3 81.4 %while.10 = (s32[]{:T(128)}, bf16[8,512,64]{1,2,0:T(8,128)(2,1)S(1)}, s32[8]{0:T(128)S(1)}, s32[4096]{0:T(1024)S(1)}, s32[16,256]{1,0:T(8,128)S(1)}, /*index=5*/...) while((s32[]{:T(128)}, ...), condition=%wide.region_5.6_spmd, body=%wide.region_2.5_spmd.sunk | while | flops 570489856 | bytes 26513576 | solution.py:131
  194.4 2.6 fusion.51
  204.6 2.6 fusion.51
  214.8 2.6 fusion.51
  224.9 2.6 fusion.51
  235.1 2.6 fusion.51
  245.3 2.6 fusion.51
  255.4 2.6 fusion.51
  265.6 2.6 fusion.51
  272.2 6.7 %all-to-all-start.4 = ((bf16[16,256,64]{1,2,0:T(8,128)(2,1)}), bf16[16,256,64]{1,2,0:T(8,128)(2,1)}, u32[]{:S(2)}, u32[]{:S(2)}) async-start(bf16[16,256,64]{1,2,0:T(8,128)(2,1)} %copy.50), calls=%async_computation.4 | async-start | bytes 1048576 | tf_op jit(solution)/shard_map/all_to_all | solution.py:132
  282.5 28.6 %all-gather.10.cloned.1.call-done = bf16[8,512,128]{2,1,0:T(8,128)(2,1)} async-done(((bf16[2,512,128]{2,1,0:T(8,128)(2,1)}), bf16[8,512,128]{2,1,0:T(8,128)(2,1)}) %all-gather.10.cloned.1.call-update) | async-done | bytes 1048592 | tf_op jit(solution)/shard_map/all_gather | solution.py:37
  311.0 2.7 maximum_bitcast_fusion
  313.8 2.9 copy.52
  316.6 2.6 fusion.29
  (77 shorter events, 60.6 us)
Async XLA Ops:
  7.4 27.5 %copy-start = (bf16[64,1024]{1,0:T(8,128)(2,1)S(1)}, bf16[64,1024]{1,0:T(8,128)(2,1)}, u32[]{:S(2)}) copy-start(bf16[64,1024]{1,0:T(8,128)(2,1)} %param.16) | copy-start | bytes 393220
  7.4 62.8 %all-gather.6.cloned.1.call-start = ((), (), s32[]{:S(2)}) async-start(), calls=%async_computation.5 | async-start | bytes 7077888 | tf_op jit(solution)/shard_map/all_gather | solution.py:88
  9.5 66.6 %all-to-all-start = ((s32[16,1,256]{2,1,0:T(1,128)}), s32[16,1,256]{2,1,0:T(1,128)S(1)}, u32[]{:S(2)}, u32[]{:S(2)}) async-start(s32[16,1,256]{2,1,0:T(1,128)} %broadcast_in_dim.31), calls=%async_computation | async-start | bytes 32768 | tf_op jit(solution)/shard_map/all_to_all | solution.py:22
  74.9 85.0 %copy-start.1 = (bf16[1024,128]{1,0:T(8,128)(2,1)S(1)}, bf16[1024,128]{1,0:T(8,128)(2,1)}, u32[]{:S(2)}) copy-start(bf16[1024,128]{1,0:T(8,128)(2,1)} %param.19) | copy-start | bytes 786436
  76.1 41.4 %all-to-all-start.1 = ((bf16[256,16,64]{0,2,1:T(8,128)(2,1)}), bf16[256,16,64]{0,2,1:T(8,128)(2,1)S(1)}, u32[]{:S(2)}, u32[]{:S(2)}) async-start(bf16[256,16,64]{0,2,1:T(8,128)(2,1)} %bitcast.12), calls=%async_computation.1 | async-start | bytes 1048576 | tf_op jit(solution)/shard_map/all_to_all | solution.py:95
  117.5 35.7 %all-to-all-start.2 = ((bf16[256,16,64]{0,2,1:T(8,128)(2,1)}), bf16[256,16,64]{0,2,1:T(8,128)(2,1)S(1)}, u32[]{:S(2)}, u32[]{:S(2)}) async-start(bf16[256,16,64]{0,2,1:T(8,128)(2,1)} %bitcast.15), calls=%async_computation.2 | async-start | bytes 1048576 | tf_op jit(solution)/shard_map/all_to_all | solution.py:96
  153.2 35.6 %all-to-all-start.3 = ((bf16[256,16,64]{0,2,1:T(8,128)(2,1)}), bf16[256,16,64]{0,2,1:T(8,128)(2,1)S(1)}, u32[]{:S(2)}, u32[]{:S(2)}) async-start(bf16[256,16,64]{0,2,1:T(8,128)(2,1)} %bitcast.17), calls=%async_computation.3 | async-start | bytes 1048576 | tf_op jit(solution)/shard_map/all_to_all | solution.py:97
  159.8 121.3 %all-gather.8.cloned.1.call-start = ((), (), s32[]{:S(2)}) async-start(), calls=%async_computation.6 | async-start | bytes 1572864 | tf_op jit(solution)/shard_map/all_gather | solution.py:37
  272.2 44.5 %all-to-all-start.4 = ((bf16[16,256,64]{1,2,0:T(8,128)(2,1)}), bf16[16,256,64]{1,2,0:T(8,128)(2,1)}, u32[]{:S(2)}, u32[]{:S(2)}) async-start(bf16[16,256,64]{1,2,0:T(8,128)(2,1)} %copy.50), calls=%async_computation.4 | async-start | bytes 1048576 | tf_op jit(solution)/shard_map/all_to_all | solution.py:132
  278.8 32.2 %all-gather.10.cloned.1.call-start = ((), (), s32[]{:S(2)}) async-start(), calls=%async_computation.7 | async-start | bytes 1310720 | tf_op jit(solution)/shard_map/all_gather | solution.py:37
Sparse Core Ops, SparseCore 0:
  10.1 60.1 all-gather.5
Sparse Core Ops, SparseCore 1:
  174.5 17.2 all-gather.7
  281.2 29.8 all-gather.9
where the time goes:
time: 328 us; the launch traced here: 327 us
  waiting for transfers between devices  132 us (40%)
  starting transfers between devices  56.5 us (17%)
  matrix products  49.5 us (15%)
  other arithmetic  23.6 us (7%)
  local copies, waits for them, and re-layouts  17.8 us (5%)
  blocking collectives  16.6 us (5%)
  loops' own time  15.8 us (5%)
  between operations  15.1 us (5%)
    all_gather x1, waiting for transfers between devices, body(): lax.all_gather(qkv_weight, FSDP, axis=0, tiled=True)  33.9 us
    all_gather x2, waiting for transfers between devices, stacked_from(): blocks = lax.all_gather(blocks, axes[k], axis=0, tiled=True)  28.6 us
    all_to_all x1, waiting for transfers between devices, body(): lax.all_to_all(queries, 'ctx', split_axis=1, concat_axis=0, tiled=True)  28 us
    all_to_all x1, waiting for transfers between devices, body(): lax.all_to_all(key_rows, 'ctx', split_axis=1, concat_axis=0, tiled=True)  27.9 us
    all_to_all x1, starting transfers between devices, sent_to_all(): return lax.all_to_all(copies, axis, split_axis=0, concat_axis=0, tiled=True)  24 us
    reduce_sum x8, other arithmetic, attend_span(): row_sums = jnp.sum(raised, axis=-1)  20.6 us
    dot_general x8, matrix products, attend_span(): jnp.einsum('hqk,khd->qhd', raised.astype(jnp.bfloat16), value_heads, pref...  20.1 us
    dot_general x8, matrix products, attend_span(): jnp.einsum('qhd,khd->hqk', span_rows, key_heads, preferred_element_type=j...  19.5 us
  transfers between devices with their start and end apart: 8, of which 5 were waited for; matrix products, arithmetic and copies ran while one was open for 27% of the time, Pallas kernels for 0%

commit v1 on v0

--- a/solution.py
+++ b/solution.py
@@ -85,7 +85,9 @@
     normed = (centered * lax.rsqrt(variance + epsilon) * norm_gain).astype(jnp.bfloat16)
     qkv = jnp.dot(
         normed,
-        lax.all_gather(qkv_weight, FSDP, axis=0, tiled=True),
+        jnp.concatenate(
+            lax.all_to_all(jnp.stack([qkv_weight] * lax.axis_size(FSDP)), FSDP, 0, 0), axis=0
+        ),
         preferred_element_type=jnp.float32,
     ).astype(jnp.bfloat16)
     queries = qkv[:, :model_width]

time: 328 us -> 367 us (1.12)
  waiting for transfers between devices: 132 us -> 172 us
  local copies, waits for them, and re-layouts: 17.8 us -> 21.8 us
    all_to_all x0 -> x1, waiting for transfers between devices: none -> 70.9 us  [body(): lax.all_to_all(jnp.stack([qkv_weight] * lax.axis_size(FSDP)), FSDP, 0, 0)]
    all_gather x1 -> x0, waiting for transfers between devices: 33.9 us -> none  [body(): lax.all_gather(qkv_weight, FSDP, axis=0, tiled=True)]
    all_to_all x1, starting transfers between devices: 12.4 us -> 5.56 us  [body(): lax.all_to_all(queries, 'ctx', split_axis=1, concat_axis=0, tiled=True)]
    all_to_all x1, waiting for transfers between devices: 0.01 us -> 6.48 us  [sent_to_all(): return lax.all_to_all(copies, axis, split_axis=0, concat_axis=0, tiled=True)]
    all_to_all x0 -> x1, starting transfers between devices: none -> 5.06 us  [body(): lax.all_to_all(jnp.stack([qkv_weight] * lax.axis_size(FSDP)), FSDP, 0, 0)]
    another operation x0 -> x1, local copies, waits for them, and re-layouts: none -> 4.66 us  [body(): jnp.stack([qkv_weight] * lax.axis_size(FSDP))]
  transfers between devices with their start and end apart: 8 -> 8, of which waited for: 5 -> 6; matrix products, arithmetic and copies ran while one was open for 27% -> 23% of each run, Pallas kernels for 0% -> 0%
where the time goes in v1:
time: 367 us; the launch traced here: 366 us
  waiting for transfers between devices  172 us (47%)
  starting transfers between devices  54.9 us (15%)
  matrix products  47.7 us (13%)
  other arithmetic  23.6 us (6%)
  local copies, waits for them, and re-layouts  21.8 us (6%)
  blocking collectives  16.6 us (5%)
  loops' own time  15.8 us (4%)
  between operations  13.7 us (4%)
    all_to_all x1, waiting for transfers between devices, body(): lax.all_to_all(jnp.stack([qkv_weight] * lax.axis_size(FSDP)), FSDP, 0, 0)  70.9 us
    all_gather x2, waiting for transfers between devices, stacked_from(): blocks = lax.all_gather(blocks, axes[k], axis=0, tiled=True)  28.3 us
    all_to_all x1, waiting for transfers between devices, body(): lax.all_to_all(key_rows, 'ctx', split_axis=1, concat_axis=0, tiled=True)  27.4 us
    all_to_all x1, waiting for transfers between devices, body(): lax.all_to_all(queries, 'ctx', split_axis=1, concat_axis=0, tiled=True)  26.7 us
    all_to_all x1, starting transfers between devices, sent_to_all(): return lax.all_to_all(copies, axis, split_axis=0, concat_axis=0, tiled=True)  24 us
    reduce_sum x8, other arithmetic, attend_span(): row_sums = jnp.sum(raised, axis=-1)  20.6 us
    dot_general x8, matrix products, attend_span(): jnp.einsum('hqk,khd->qhd', raised.astype(jnp.bfloat16), value_heads, pref...  20.1 us
    dot_general x8, matrix products, attend_span(): jnp.einsum('qhd,khd->hqk', span_rows, key_heads, preferred_element_type=j...  19.6 us
  transfers between devices with their start and end apart: 8, of which 6 were waited for; matrix products, arithmetic and copies ran while one was open for 23% of the time, Pallas kernels for 0%

profile of v1, /device:TPU:40, one launch (start us, length us, event | category | flops | bytes accessed | tf_op | source)
XLA Modules:
  0.0 365.8 jit_solution(1661031329398723167)
XLA Ops:
  6.6 4.7 %stack.2 = bf16[8,128,3072]{2,1,0:T(8,128)(2,1)} broadcast(bf16[128,3072]{1,0:T(8,128)(2,1)} %param.18), dimensions={1,2} | broadcast | bytes 7077888 | tf_op jit(solution)/shard_map/stack | solution.py:89
  11.2 5.1 %all-to-all-start.1 = ((bf16[8,128,3072]{2,1,0:T(8,128)(2,1)}), bf16[8,128,3072]{2,1,0:T(8,128)(2,1)}, u32[]{:S(2)}, u32[]{:S(2)}) async-start(bf16[8,128,3072]{2,1,0:T(8,128)(2,1)} %stack.2), calls=%async_computation.1 | async-start | bytes 12582912 | tf_op jit(solution)/shard_map/all_to_all | solution.py:89
  17.4 70.9 %all-to-all-done.1 = bf16[8,128,3072]{2,1,0:T(8,128)(2,1)} async-done(((bf16[8,128,3072]{2,1,0:T(8,128)(2,1)}), bf16[8,128,3072]{2,1,0:T(8,128)(2,1)}, u32[]{:S(2)}, u32[]{:S(2)}) %all-to-all-start.1) | async-done | bytes 6291488 | tf_op jit(solution)/shard_map/all_to_all | solution.py:89
  88.9 24.0 %all-to-all-start = ((s32[16,1,256]{2,1,0:T(1,128)}), s32[16,1,256]{2,1,0:T(1,128)S(1)}, u32[]{:S(2)}, u32[]{:S(2)}) async-start(s32[16,1,256]{2,1,0:T(1,128)} %broadcast_in_dim.31), calls=%async_computation | async-start | bytes 32768 | tf_op jit(solution)/shard_map/all_to_all | solution.py:22
  112.9 4.7 %convolution_convert_fusion = bf16[256,3072]{1,0:T(8,128)(2,1)S(1)} fusion(bf16[1024,3072]{1,0:T(8,128)(2,1)} %bitcast.12, f32[256,1024]{1,0:T(8,128)S(1)} %get-tuple-element.96, f32[1024]{0:T(1024)S(1)} %copy-done.7, f32[256]{0:T(256)S(1)} %add_rsqrt_fusion, f32[256]{0:T(256)S(1)} %broadcast_multiply_fusion), kind=kOutput, calls=%fused_computation.19 | convolution fusion | flops 1612447744 | bytes 8919040 | tf_op jit(solution)/shard_map/dot_general | solution.py:86
  118.7 6.5 %all-to-all-done = s32[16,1,256]{2,1,0:T(1,128)S(1)} async-done(((s32[16,1,256]{2,1,0:T(1,128)}), s32[16,1,256]{2,1,0:T(1,128)S(1)}, u32[]{:S(2)}, u32[]{:S(2)}) %all-to-all-start) | async-done | bytes 16416 | tf_op jit(solution)/shard_map/all_to_all | solution.py:22
  125.2 5.6 %all-to-all-start.2 = ((bf16[256,16,64]{0,2,1:T(8,128)(2,1)}), bf16[256,16,64]{0,2,1:T(8,128)(2,1)S(1)}, u32[]{:S(2)}, u32[]{:S(2)}) async-start(bf16[256,16,64]{0,2,1:T(8,128)(2,1)} %bitcast.13), calls=%async_computation.2 | async-start | bytes 1048576 | tf_op jit(solution)/shard_map/all_to_all | solution.py:97
  131.8 26.7 %all-to-all-done.2 = bf16[256,16,64]{0,2,1:T(8,128)(2,1)S(1)} async-done(((bf16[256,16,64]{0,2,1:T(8,128)(2,1)}), bf16[256,16,64]{0,2,1:T(8,128)(2,1)S(1)}, u32[]{:S(2)}, u32[]{:S(2)}) %all-to-all-start.2) | async-done | bytes 524320 | tf_op jit(solution)/shard_map/all_to_all | solution.py:97
  158.5 6.8 %all-to-all-start.3 = ((bf16[256,16,64]{0,2,1:T(8,128)(2,1)}), bf16[256,16,64]{0,2,1:T(8,128)(2,1)S(1)}, u32[]{:S(2)}, u32[]{:S(2)}) async-start(bf16[256,16,64]{0,2,1:T(8,128)(2,1)} %bitcast.16), calls=%async_computation.3 | async-start | bytes 1048576 | tf_op jit(solution)/shard_map/all_to_all | solution.py:98
  166.3 27.4 %all-to-all-done.3 = bf16[256,16,64]{0,2,1:T(8,128)(2,1)S(1)} async-done(((bf16[256,16,64]{0,2,1:T(8,128)(2,1)}), bf16[256,16,64]{0,2,1:T(8,128)(2,1)S(1)}, u32[]{:S(2)}, u32[]{:S(2)}) %all-to-all-start.3) | async-done | bytes 524320 | tf_op jit(solution)/shard_map/all_to_all | solution.py:98
  193.8 6.6 %all-to-all-start.4 = ((bf16[256,16,64]{0,2,1:T(8,128)(2,1)}), bf16[256,16,64]{0,2,1:T(8,128)(2,1)S(1)}, u32[]{:S(2)}, u32[]{:S(2)}) async-start(bf16[256,16,64]{0,2,1:T(8,128)(2,1)} %bitcast.18), calls=%async_computation.4 | async-start | bytes 1048576 | tf_op jit(solution)/shard_map/all_to_all | solution.py:99
  200.5 14.4 %all-gather = bf16[2048,128]{1,0:T(8,128)(2,1)} all-gather(bf16[512,128]{1,0:T(8,128)(2,1)S(1)} %get-tuple-element.93), channel_id=2, replica_groups=mesh['groups'=2,'ctx'=16,'fsdp_0'=4,'fsdp_1'=2] {'fsdp_0'}, dimensions={0}, use_global_device_ids=true | all-gather | bytes 655360 | tf_op jit(solution)/shard_map/all_gather | solution.py:37
  216.9 11.8 %all-to-all-done.4 = bf16[256,16,64]{0,2,1:T(8,128)(2,1)S(1)} async-done(((bf16[256,16,64]{0,2,1:T(8,128)(2,1)}), bf16[256,16,64]{0,2,1:T(8,128)(2,1)S(1)}, u32[]{:S(2)}, u32[]{:S(2)}) %all-to-all-start.4) | async-done | bytes 524320 | tf_op jit(solution)/shard_map/all_to_all | solution.py:99
  229.3 81.4 %while.10 = (s32[]{:T(128)}, bf16[8,512,64]{1,2,0:T(8,128)(2,1)S(1)}, s32[8]{0:T(128)S(1)}, s32[4096]{0:T(1024)S(1)}, s32[16,256]{1,0:T(8,128)S(1)}, /*index=5*/...) while((s32[]{:T(128)}, ...), condition=%wide.region_5.6_spmd, body=%wide.region_2.5_spmd.sunk | while | flops 570489856 | bytes 26513576 | solution.py:133
  234.4 2.6 fusion.51
  244.5 2.6 fusion.51
  254.7 2.6 fusion.51
  264.9 2.6 fusion.51
  295.4 2.6 fusion.51
  312.1 6.7 %all-to-all-start.5 = ((bf16[16,256,64]{1,2,0:T(8,128)(2,1)}), bf16[16,256,64]{1,2,0:T(8,128)(2,1)}, u32[]{:S(2)}, u32[]{:S(2)}) async-start(bf16[16,256,64]{1,2,0:T(8,128)(2,1)} %copy.50), calls=%async_computation.5 | async-start | bytes 1048576 | tf_op jit(solution)/shard_map/all_to_all | solution.py:134
  322.5 28.3 %all-gather.7.cloned.1.call-done = bf16[8,512,128]{2,1,0:T(8,128)(2,1)} async-done(((bf16[2,512,128]{2,1,0:T(8,128)(2,1)}), bf16[8,512,128]{2,1,0:T(8,128)(2,1)}) %all-gather.7.cloned.1.call-update) | async-done | bytes 1048592 | tf_op jit(solution)/shard_map/all_gather | solution.py:37
  350.8 2.7 maximum_bitcast_fusion
  353.5 2.9 copy.52
  356.4 2.6 fusion.29
  (89 shorter events, 65.2 us)
Async XLA Ops:
  6.5 10.1 %copy-start = (bf16[64,1024]{1,0:T(8,128)(2,1)S(1)}, bf16[64,1024]{1,0:T(8,128)(2,1)}, u32[]{:S(2)}) copy-start(bf16[64,1024]{1,0:T(8,128)(2,1)} %param.16) | copy-start | bytes 393220
  6.6 9.8 %copy-start.5 = (s32[1,256]{1,0:T(1,128)S(1)}, s32[1,256]{1,0:T(1,128)}, u32[]{:S(2)}) copy-start(s32[1,256]{1,0:T(1,128)} %param.13) | copy-start | bytes 3076
  6.6 9.8 %copy-start.1 = (bf16[1,256,1024]{2,1,0:T(8,128)(2,1)S(1)}, bf16[1,256,1024]{2,1,0:T(8,128)(2,1)}, u32[]{:S(2)}) copy-start(bf16[1,256,1024]{2,1,0:T(8,128)(2,1)} %param.11) | copy-start | bytes 1572868
  6.6 9.8 %copy-start.3 = (bf16[64,1024]{1,0:T(8,128)(2,1)S(1)}, bf16[64,1024]{1,0:T(8,128)(2,1)}, u32[]{:S(2)}) copy-start(bf16[64,1024]{1,0:T(8,128)(2,1)} %param.15) | copy-start | bytes 393220
  11.2 5.5 %copy-start.4 = (s32[1,256]{1,0:T(1,128)S(1)}, s32[1,256]{1,0:T(1,128)}, u32[]{:S(2)}) copy-start(s32[1,256]{1,0:T(1,128)} %param.14) | copy-start | bytes 3076
  11.2 77.1 %copy-start.6 = (s32[1,256]{1,0:T(1,128)S(1)}, s32[1,256]{1,0:T(1,128)}, u32[]{:S(2)}) copy-start(s32[1,256]{1,0:T(1,128)} %param.12) | copy-start | bytes 3076
  11.2 101.7 %copy-start.7 = (f32[1024]{0:T(1024)S(1)}, f32[1024]{0:T(1024)}, u32[]{:S(2)}) copy-start(f32[1024]{0:T(1024)} %param.17) | copy-start | bytes 12292
  11.2 77.1 %all-to-all-start.1 = ((bf16[8,128,3072]{2,1,0:T(8,128)(2,1)}), bf16[8,128,3072]{2,1,0:T(8,128)(2,1)}, u32[]{:S(2)}, u32[]{:S(2)}) async-start(bf16[8,128,3072]{2,1,0:T(8,128)(2,1)} %stack.2), calls=%async_computation.1 | async-start | bytes 12582912 | tf_op jit(solution)/shard_map/all_to_all | solution.py:89
  88.9 36.3 %all-to-all-start = ((s32[16,1,256]{2,1,0:T(1,128)}), s32[16,1,256]{2,1,0:T(1,128)S(1)}, u32[]{:S(2)}, u32[]{:S(2)}) async-start(s32[16,1,256]{2,1,0:T(1,128)} %broadcast_in_dim.31), calls=%async_computation | async-start | bytes 32768 | tf_op jit(solution)/shard_map/all_to_all | solution.py:22
  117.6 82.9 %copy-start.2 = (bf16[1024,128]{1,0:T(8,128)(2,1)S(1)}, bf16[1024,128]{1,0:T(8,128)(2,1)}, u32[]{:S(2)}) copy-start(bf16[1024,128]{1,0:T(8,128)(2,1)} %param.19) | copy-start | bytes 786436
  125.2 33.3 %all-to-all-start.2 = ((bf16[256,16,64]{0,2,1:T(8,128)(2,1)}), bf16[256,16,64]{0,2,1:T(8,128)(2,1)S(1)}, u32[]{:S(2)}, u32[]{:S(2)}) async-start(bf16[256,16,64]{0,2,1:T(8,128)(2,1)} %bitcast.13), calls=%async_computation.2 | async-start | bytes 1048576 | tf_op jit(solution)/shard_map/all_to_all | solution.py:97
  158.5 35.3 %all-to-all-start.3 = ((bf16[256,16,64]{0,2,1:T(8,128)(2,1)}), bf16[256,16,64]{0,2,1:T(8,128)(2,1)S(1)}, u32[]{:S(2)}, u32[]{:S(2)}) async-start(bf16[256,16,64]{0,2,1:T(8,128)(2,1)} %bitcast.16), calls=%async_computation.3 | async-start | bytes 1048576 | tf_op jit(solution)/shard_map/all_to_all | solution.py:98
  193.8 35.0 %all-to-all-start.4 = ((bf16[256,16,64]{0,2,1:T(8,128)(2,1)}), bf16[256,16,64]{0,2,1:T(8,128)(2,1)S(1)}, u32[]{:S(2)}, u32[]{:S(2)}) async-start(bf16[256,16,64]{0,2,1:T(8,128)(2,1)} %bitcast.18), calls=%async_computation.4 | async-start | bytes 1048576 | tf_op jit(solution)/shard_map/all_to_all | solution.py:99
  200.4 120.8 %all-gather.5.cloned.1.call-start = ((), (), s32[]{:S(2)}) async-start(), calls=%async_computation.6 | async-start | bytes 1572864 | tf_op jit(solution)/shard_map/all_gather | solution.py:37
  312.1 44.2 %all-to-all-start.5 = ((bf16[16,256,64]{1,2,0:T(8,128)(2,1)}), bf16[16,256,64]{1,2,0:T(8,128)(2,1)}, u32[]{:S(2)}, u32[]{:S(2)}) async-start(bf16[16,256,64]{1,2,0:T(8,128)(2,1)} %copy.50), calls=%async_computation.5 | async-start | bytes 1048576 | tf_op jit(solution)/shard_map/all_to_all | solution.py:134
  318.9 32.0 %all-gather.7.cloned.1.call-start = ((), (), s32[]{:S(2)}) async-start(), calls=%async_computation.7 | async-start | bytes 1310720 | tf_op jit(solution)/shard_map/all_gather | solution.py:37
Sparse Core Ops, SparseCore 0:
  215.1 17.2 all-gather.4
  321.5 29.2 all-gather.6
